TPU v7x, 32 devices: a whole 2x2x4 slice. The times are simulated.
32 devices in a mesh: seq: 8 (over z, y), head: 4 (over x, core).
Axes of the slice: x: 2, y: 2, z: 4, core: 2. Of those that a mesh axis runs over, the one named last changes fastest.
Arguments:
- inputs: bfloat16 [2048, 5120], P('seq', 'head'), may hold values from -6 to 6
- time_step: float32 [80, 2048], P('head', 'seq'), may hold values from 0.01 to 0.3
- decay_rate: float32 [80], P('head'), may hold values from 0.0001 to 1
- input_map: bfloat16 [2048, 128], P('seq'), may hold values from -6 to 6
- output_map: bfloat16 [2048, 128], P('seq'), may hold values from -0.59765625 to 0.59765625
- output_grad: bfloat16 [2048, 5120], P('seq', 'head'), may hold values from -3 to 3
- span_states: float32 [8, 80, 64, 128], P('seq', 'head'), may hold values from -6 to 6
- resets: int32 [8], P('seq'), may hold values from 0 to 4095
Outputs:
- grad_inputs: bfloat16 [2048, 5120], P('seq', 'head')
- grad_input_map: float32 [2048, 128], P('seq')
- grad_rate: float32 [80], P('head')
Inputs may be any that keep to these rules, and one draw needn't show every extreme that they name: `resets`: A value p under 256 means that a document starts at position p of that span; a value of 256 or more means that none starts in it.
All inputs are finite; a program needn't handle non-finite values.
Results may differ from a plain program's by a relative error of at most 0.003.
Values sent between devices are 32-bit elements; how exact they have to be, the bound alone decides.
A program may use at most 64 MiB of HBM per device.

v0:
```python
import jax
import jax.numpy as jnp
from jax import lax
from jax.sharding import PartitionSpec as P

highest = lax.Precision.HIGHEST


def prepare(x_block, step_block, decay_rate, b_block, c_block, grad_block, start_state, reset_at):
    block_len = step_block.shape[1]
    positions = jnp.arange(block_len, dtype=jnp.int32)
    later_doc = positions >= reset_at
    no_reset = reset_at >= block_len
    elapsed = jnp.cumsum(step_block, axis=1)
    log_decay = -decay_rate[:, None] * elapsed
    joined = (later_doc[:, None] == later_doc[None, :]) & (positions[None, :] >= positions[:, None])
    log_gaps = log_decay[:, None, :] - log_decay[:, :, None]
    pair_weight = jnp.where(joined[None], jnp.exp(jnp.where(joined[None], log_gaps, 0.0)), 0.0)
    intersection = jnp.dot(b_block, c_block.T, preferred_element_type=jnp.float32)
    products = jnp.einsum("shp,uhp->hsu", x_block, grad_block, preferred_element_type=jnp.float32)
    mixing = (pair_weight * intersection[None]).astype(jnp.bfloat16)
    pair_terms = pair_weight * products
    paired = pair_terms.astype(jnp.bfloat16)
    dx_inner = jnp.einsum("hsu,uhp->shp", mixing, grad_block, preferred_element_type=jnp.float32)
    db_inner = jnp.einsum("hsu,un->hsn", paired, c_block, preferred_element_type=jnp.float32)
    start_weight = jnp.where(later_doc[None], 0.0, jnp.exp(log_decay))
    end_weight = jnp.where(
        (later_doc | no_reset)[None], jnp.exp(log_decay[:, -1:] - log_decay), 0.0
    )
    carry_gain = jnp.where(no_reset, jnp.exp(log_decay[:, -1]), 0.0)
    c_wide = c_block.astype(jnp.float32)
    grad_wide = grad_block.astype(jnp.float32)
    weighted_c = start_weight[:, :, None] * c_wide[None]
    boundary_grad = jnp.einsum("hun,uhp->hpn", weighted_c, grad_wide, precision=highest)
    state_read = jnp.einsum("uhp,hpn->hun", grad_wide, start_state, precision=highest)
    start_term = jnp.sum(state_read * c_wide[None], axis=2)
    inside_term = jnp.sum(
        pair_terms
        * intersection[None]
        * step_block[:, :, None]
        * (elapsed[:, None, :] - elapsed[:, :, None]),
        axis=(1, 2),
    )
    entry_term = jnp.sum(start_weight * elapsed * start_term, axis=1)
    return (
        carry_gain,
        boundary_grad,
        dx_inner,
        db_inner,
        inside_term + entry_term,
        end_weight,
        elapsed,
    )


def finish(prepared, x_block, step_block, b_block, start_state, carried):
    carry_gain, boundary_grad, dx_inner, db_inner, partial_rate, end_weight, elapsed = prepared
    b_wide = b_block.astype(jnp.float32)
    x_wide = x_block.astype(jnp.float32)
    carried_b = jnp.einsum("sn,hpn->shp", b_wide, carried, precision=highest)
    carried_x = jnp.einsum("shp,hpn->hsn", x_wide, carried, precision=highest)
    step_rows = step_block.T[:, :, None]
    end_rows = end_weight.T[:, :, None]
    grad_x = (step_rows * (dx_inner + end_rows * carried_b)).astype(jnp.bfloat16)
    grad_b = jnp.sum(
        step_block[:, :, None] * (db_inner + end_weight[:, :, None] * carried_x), axis=0
    )
    last_elapsed = elapsed[:, -1]
    leaving_term = jnp.sum(
        end_weight
        * step_block
        * (last_elapsed[:, None] - elapsed)
        * jnp.sum(carried_x * b_wide[None], axis=2),
        axis=1,
    )
    through_term = carry_gain * last_elapsed * jnp.sum(carried * start_state, axis=(1, 2))
    return (grad_x, grad_b, partial_rate + leaving_term + through_term)


def backward_step(running, members):
    grad_piece, gain_piece = members
    return (grad_piece + gain_piece[:, None] * running, running)


def body(inputs, time_step, decay_rate, input_map, output_map, output_grad, span_states, resets):
    length = time_step.shape[1]
    block_count = span_states.shape[0]
    block_len = length // block_count
    head_count = decay_rate.shape[0]
    head_width = inputs.shape[1] // head_count
    number = 0
    x_block = inputs.reshape(block_len, head_count, head_width)
    grad_block = output_grad.reshape(block_len, head_count, head_width)
    step_block = time_step
    b_block = input_map
    prepared = prepare(
        x_block,
        step_block,
        decay_rate,
        b_block,
        output_map,
        grad_block,
        span_states[number],
        resets[number],
    )
    pieces = [(prepared, x_block, step_block, b_block)]
    gain_total = jnp.ones((head_count,), jnp.float32)
    grad_total = jnp.zeros_like(span_states[0])
    for number in reversed(range(block_count)):
        gain_block, grad_block_sum = (pieces[number][0][0], pieces[number][0][1])
        grad_total = grad_block_sum + gain_block[:, None, None] * grad_total
        gain_total = gain_block * gain_total
    seq_count = lax.axis_size("seq")
    entries = grad_total.shape[1] * grad_total.shape[2]
    sliced = grad_total.reshape(head_count, seq_count, entries // seq_count)
    received = lax.all_to_all(sliced, "seq", split_axis=1, concat_axis=1, tiled=True)
    gains = lax.all_gather(gain_total[None], "seq", axis=0, tiled=True)
    ending, exclusive = lax.scan(
        backward_step,
        jnp.zeros_like(received[:, 0]),
        (jnp.transpose(received, (1, 0, 2)), gains),
        reverse=True,
    )
    returned = lax.all_to_all(
        jnp.transpose(exclusive, (1, 0, 2)), "seq", split_axis=1, concat_axis=1, tiled=True
    )
    incoming = returned.reshape(grad_total.shape)
    carried = incoming
    grad_x_list = [None] * block_count
    grad_b_list = [None] * block_count
    rate_total = jnp.zeros((head_count,), jnp.float32)
    for number in reversed(range(block_count)):
        prepared, x_block, step_block, b_block = pieces[number]
        grad_x, grad_b, rate_part = finish(
            prepared, x_block, step_block, b_block, span_states[number], carried
        )
        grad_x_list[number] = grad_x.reshape(block_len, head_count * head_width)
        grad_b_list[number] = grad_b
        rate_total = rate_part
        carried = prepared[1] + prepared[0][:, None, None] * carried
    grad_inputs = grad_x_list[0]
    grad_input_map = lax.psum(grad_b_list[0], "head")
    grad_rate = -lax.psum(rate_total, "seq")
    return (grad_inputs, grad_input_map, grad_rate)


def solution(mesh):
    in_specs = (
        P("seq", "head"),
        P("head", "seq"),
        P("head"),
        P("seq", None),
        P("seq", None),
        P("seq", "head"),
        P("seq", "head", None, None),
        P("seq"),
    )
    out_specs = (P("seq", "head"), P("seq", None), P("head"))
    return jax.shard_map(body, mesh=mesh, in_specs=in_specs, out_specs=out_specs, check_vma=False)
```

profile of v0, /device:TPU:0, one launch (start us, length us, event | category | flops | bytes accessed | tf_op | source)
XLA Modules:
  0.0 141.0 jit_solution(17333116644024165966)
XLA Ops:
  8.0 0.7 neg.7
  8.6 0.8 reshape.290
  9.4 0.6 reduce-window.6
  10.3 0.6 iota_compare_fusion.1
  11.2 0.9 copy.37
  12.2 1.4 copy.36
  13.6 1.7 %fusion.31 = f32[20,64,128]{2,1,0:T(8,128)S(1)} fusion(bf16[256,20,64]{0,2,1:T(8,128)(2,1)S(1)} %bitcast.80, f32[256,128]{0,1:T(8,128)S(1)} %copy.37, f32[20,256]{1,0:T(8,128)S(1)} %get-tuple-element.152, f32[20]{0:T(128)S(1)} %broadcast_multiply_fusion.1), kind=kOutput, calls=%fused_computation.38 | convolution fusion | flops 504135680 | bytes 1462352 | tf_op jit(solution)/shard_map/hun,uhp->hpn/dot_general | solution.py:34
  15.4 1.3 copy.39
  16.7 7.3 %all-to-all-start = ((f32[20,8,1024]{2,0,1:T(8,128)}), f32[20,8,1024]{2,0,1:T(8,128)S(1)}, u32[]{:S(2)}, u32[]{:S(2)}) async-start(f32[20,8,1024]{2,0,1:T(8,128)} %copy.39), calls=%async_computation | async-start | bytes 1572864 | tf_op jit(solution)/shard_map/all_to_all | solution.py:116
  24.0 0.6 dynamic-slice
  25.6 26.1 %all-reduce = f32[160]{0:T(256)S(1)} all-reduce(f32[160]{0:T(256)S(1)} %dynamic-update-slice), channel_id=2, replica_groups=mesh['seq'=8,'head'=4] {'seq'}, use_global_device_ids=true, to_apply=%add | all-reduce | flops 160 | bytes 1280
  51.7 0.7 reshape.297
  52.3 0.7 convert_element_type.21
  53.4 0.6 compare_bitcast_fusion
  53.9 0.7 slice_reduce_fusion.1
  54.7 1.4 %fusion.37 = pred[256,256]{1,0:T(8,128)(4,1)} fusion(pred[256]{0:T(512)(128)(4,1)} %copy-done.10), kind=kLoop, calls=%fused_computation.42 | loop fusion | flops 196608 | bytes 65792 | tf_op jit(solution)/shard_map/and | solution.py:16
  56.1 1.8 %fusion.43 = f32[256,256]{1,0:T(8,128)} fusion(bf16[256,128]{1,0:T(8,128)(2,1)} %param.13, bf16[256,128]{1,0:T(8,128)(2,1)} %param.14), kind=kOutput, calls=%fused_computation.64 | convolution fusion | flops 16777216 | bytes 393216 | tf_op jit(solution)/shard_map/dot_general | solution.py:19
  57.9 1.0 broadcast_in_dim.97
  58.9 11.4 %while.17 = (s32[]{:T(128)}, f32[20,1024]{1,0:T(8,128)S(1)}, f32[8,20,1024]{2,1,0:T(8,128)}, f32[8,20,1024]{2,1,0:T(8,128)S(1)}, f32[8,20]{1,0:T(8,128)}, /*index=5*/s32[]{:T(128)}, s32[]{:T(128)}, s32[]{:T(128)}) while((s32[]{:T(128)}, f32[20,1024]{1,0:T(8,128)S(1)}, f32[8,20,1024]{2,1,0:T(8,128)}, f32[8,20,1024]{2,1,0:T(8,128)S(1)}, ...), condition=%wide.region_3.4_spmd.clone, body=%wide.region_2.3_spmd.clone.sunk | while | flops 81924 | bytes 426352 | solution.py:118
  58.9 0.7 fusion.55
  59.5 0.6 bitcast_dynamic-update-slice_fusion.2
  60.3 0.7 fusion.55
  61.0 0.6 bitcast_dynamic-update-slice_fusion.2
  61.7 0.7 fusion.55
  62.4 0.6 bitcast_dynamic-update-slice_fusion.2
  63.1 0.7 fusion.55
  63.8 0.6 bitcast_dynamic-update-slice_fusion.2
  64.6 0.7 fusion.55
  65.2 0.6 bitcast_dynamic-update-slice_fusion.2
  66.0 0.7 fusion.55
  66.7 0.6 bitcast_dynamic-update-slice_fusion.2
  67.4 0.7 fusion.55
  68.1 0.6 bitcast_dynamic-update-slice_fusion.2
  68.9 0.7 fusion.55
  69.5 0.6 bitcast_dynamic-update-slice_fusion.2
  70.3 4.5 %all-to-all-start.1 = ((f32[20,8,1024]{2,0,1:T(8,128)}), f32[20,8,1024]{2,0,1:T(8,128)S(1)}, u32[]{:S(2)}, u32[]{:S(2)}) async-start(f32[20,8,1024]{2,0,1:T(8,128)} %bitcast.8), calls=%async_computation.1 | async-start | bytes 1572864 | tf_op jit(solution)/shard_map/all_to_all | solution.py:124
  74.8 2.8 %multiply_reduce_fusion.1 = f32[20,256]{1,0:T(8,128)} fusion(bf16[256,20,64]{0,2,1:T(8,128)(2,1)S(1)} %bitcast.81, f32[256,128]{0,1:T(8,128)} %copy-done.7, f32[1,20,64,128]{3,2,1,0:T(8,128)S(1)} %copy-done.2), kind=kOutput, calls=%fused_computation.17 | convolution fusion | flops 504622080 | bytes 1462272 | tf_op jit(solution)/shard_map/uhp,hpn->hun/dot_general | solution.py:35
  77.7 3.7 %fusion.21 = f32[256,20,64]{0,2,1:T(8,128)} fusion(bf16[256,20,64]{0,2,1:T(8,128)(2,1)S(1)} %bitcast.82, f32[256,256]{1,0:T(8,128)} %fusion.43, f32[20,256]{1,0:T(8,128)S(1)} %get-tuple-element.153, pred[256,256]{1,0:T(8,128)(4,1)} %fusion.37), kind=kOutput, calls=%fused_computation.29 | convolution fusion | flops 174325760 | bytes 2314240 | tf_op jit(solution)/shard_map/hsu,uhp->shp/dot_general | solution.py:24
  81.4 5.3 %multiply_reduce_fusion = (f32[20]{0:T(128)}, f32[20,256,256]{2,1,0:T(8,128)}) fusion(f32[20,256]{1,0:T(8,128)S(1)} %bitcast.86, f32[20,256]{1,0:T(8,128)S(1)} %copy-done.6, f32[256,256]{1,0:T(8,128)S(1)} %copy-done.5, f32[20,256]{1,0:T(8,128)S(1)} %get-tuple-element.153, pred[256,256]{1,0:T(8,128)(4,1)S(1)} %copy-done.8, ...), kind=kOutput, calls=%fused_computation.4 | convolution fusion | flops 179568624 | bytes 6942800 | tf_op jit(solution)/shard_map/shp,uhp->hsu/dot_general | solution.py:20
  86.8 5.5 %all-to-all-done.1 = f32[20,8,1024]{2,0,1:T(8,128)S(1)} async-done(((f32[20,8,1024]{2,0,1:T(8,128)}), f32[20,8,1024]{2,0,1:T(8,128)S(1)}, u32[]{:S(2)}, u32[]{:S(2)}) %all-to-all-start.1) | async-done | bytes 655392 | tf_op jit(solution)/shard_map/all_to_all | solution.py:124
  92.3 1.1 multiply_reduce_fusion.2
  93.4 2.8 %fusion.9 = (f32[20,256]{1,0:T(8,128)S(1)}, f32[20,128,256]{1,2,0:T(8,128)S(1)}) fusion(f32[256,128]{1,0:T(8,128)} %convert_element_type.21, f32[20,64,128]{2,1,0:T(8,128)S(1)} %reshape.294, bf16[256,20,64]{0,2,1:T(8,128)(2,1)S(1)} %bitcast.77), kind=kOutput, calls=%fused_computation.16 | convolution fusion | flops 504622080 | bytes 4083712 | tf_op jit(solution)/shard_map/shp,hpn->hsn/dot_general | solution.py:61
  96.5 5.2 %fusion.8 = f32[256,128]{1,0:T(8,128)} fusion(f32[20,128,256]{1,2,0:T(8,128)S(1)} %get-tuple-element.155, f32[20,256]{1,0:T(8,128)S(1)} %get-tuple-element.150, f32[20,256]{1,0:T(8,128)S(1)} %copy-done.6, f32[20,256,256]{2,1,0:T(8,128)} %get-tuple-element.157, f32[20,256]{1,0:T(8,128)S(1)} %get-tuple-element.153, pred[256,256]{1,0:T(8,128)(4,1)} %fusion.37, ...), kind=kOutput, calls=%fused_computation.15 | convolution fusion | flops 344686592 | bytes 8187904 | tf_op jit(solution)/shard_map/hsu,un->hsn/dot_general | solution.py:25
  101.8 0.7 fusion.25
  102.4 19.4 %psum.15 = f32[20]{0:T(128)S(1)} all-reduce(f32[20]{0:T(128)S(1)} %multiply_add_fusion), channel_id=1, replica_groups=mesh['seq'=8,'head'=4] {'seq'}, use_global_device_ids=true, to_apply=%region_12.13 | all-reduce | flops 20 | bytes 160 | tf_op jit(solution)/shard_map/psum | solution.py:143
  121.8 1.1 copy.44
  123.4 9.1 %all-reduce.3.cloned.1.call-done = f32[256,128]{1,0:T(8,128)} async-done(((f32[256,128]{1,0:T(8,128)}), f32[256,128]{1,0:T(8,128)}) %all-reduce.3.cloned.1.call-update) | async-done | bytes 131088 | tf_op jit(solution)/shard_map/psum | solution.py:142
  132.6 1.6 %copy.62 = f32[256,128]{1,0:T(8,128)} copy(f32[256,128]{1,0:T(8,128)} %all-reduce.3.cloned.1.call-done) | data formatting | bytes 262144
  (74 shorter events, 2.9 us)
Async XLA Ops:
  7.2 16.8 %copy-start.20 = (u32[32]{0:T(128)S(1)}, u32[32]{0:T(128)}, u32[]{:S(2)}) copy-start(u32[32]{0:T(128)} %constant.57) | copy-start | bytes 388
  7.2 45.2 %copy-start.3 = (bf16[256,128]{1,0:T(8,128)(2,1)S(1)}, bf16[256,128]{1,0:T(8,128)(2,1)}, u32[]{:S(2)}) copy-start(bf16[256,128]{1,0:T(8,128)(2,1)} %param.13) | copy-start | bytes 196612
  7.2 45.8 %copy-start.1 = (bf16[256,1280]{1,0:T(8,128)(2,1)S(1)}, bf16[256,1280]{1,0:T(8,128)(2,1)}, u32[]{:S(2)}) copy-start(bf16[256,1280]{1,0:T(8,128)(2,1)} %param.10) | copy-start | bytes 1966084
  7.2 46.0 %copy-start.2 = (f32[1,20,64,128]{3,2,1,0:T(8,128)S(1)}, f32[1,20,64,128]{3,2,1,0:T(8,128)}, u32[]{:S(2)}) copy-start(f32[1,20,64,128]{3,2,1,0:T(8,128)} %param.16) | copy-start | bytes 1966084
  8.6 43.7 %copy-start.14 = (f32[20]{0:T(128)}, f32[20]{0:T(128)S(1)}, u32[]{:S(2)}) copy-start(f32[20]{0:T(128)S(1)} %neg.7) | copy-start | bytes 244
  10.9 41.4 %copy-start.10 = (pred[256]{0:T(512)(128)(4,1)}, pred[256]{0:T(512)(128)(4,1)S(1)}, u32[]{:S(2)}) copy-start(pred[256]{0:T(512)(128)(4,1)S(1)} %get-tuple-element.158) | copy-start | bytes 772
  11.2 41.1 %copy-start.11 = (f32[20]{0:T(128)}, f32[20]{0:T(128)S(1)}, u32[]{:S(2)}) copy-start(f32[20]{0:T(128)S(1)} %get-tuple-element.137) | copy-start | bytes 244
  12.2 1.4 copy-start.7
  16.7 41.2 %all-to-all-start = ((f32[20,8,1024]{2,0,1:T(8,128)}), f32[20,8,1024]{2,0,1:T(8,128)S(1)}, u32[]{:S(2)}, u32[]{:S(2)}) async-start(f32[20,8,1024]{2,0,1:T(8,128)} %copy.39), calls=%async_computation | async-start | bytes 1572864 | tf_op jit(solution)/shard_map/all_to_all | solution.py:116
  70.3 22.0 %all-to-all-start.1 = ((f32[20,8,1024]{2,0,1:T(8,128)}), f32[20,8,1024]{2,0,1:T(8,128)S(1)}, u32[]{:S(2)}, u32[]{:S(2)}) async-start(f32[20,8,1024]{2,0,1:T(8,128)} %bitcast.8), calls=%async_computation.1 | async-start | bytes 1572864 | tf_op jit(solution)/shard_map/all_to_all | solution.py:124
  74.8 57.8 %all-reduce.3.cloned.1.call-start = ((), (), s32[]{:S(2)}) async-start(), calls=%async_computation.2 | async-start | bytes 262144 | tf_op jit(solution)/shard_map/psum | solution.py:142
  77.7 3.7 %copy-start.5 = (f32[256,256]{1,0:T(8,128)S(1)}, f32[256,256]{1,0:T(8,128)}, u32[]{:S(2)}) copy-start(f32[256,256]{1,0:T(8,128)} %fusion.43) | copy-start | bytes 786436
  77.7 3.7 %copy-start.6 = (f32[20,256]{1,0:T(8,128)S(1)}, f32[20,256]{1,0:T(8,128)}, u32[]{:S(2)}) copy-start(f32[20,256]{1,0:T(8,128)} %param.11) | copy-start | bytes 61444
  77.7 3.7 %copy-start.8 = (pred[256,256]{1,0:T(8,128)(4,1)S(1)}, pred[256,256]{1,0:T(8,128)(4,1)}, u32[]{:S(2)}) copy-start(pred[256,256]{1,0:T(8,128)(4,1)} %fusion.37) | copy-start | bytes 196612
  86.8 9.4 %copy-start.9 = (f32[20,256]{1,0:T(8,128)S(1)}, f32[20,256]{1,0:T(8,128)}, u32[]{:S(2)}) copy-start(f32[20,256]{1,0:T(8,128)} %multiply_reduce_fusion.1) | copy-start | bytes 61444
  86.8 9.4 %copy-start.12 = (f32[20]{0:T(128)S(1)}, f32[20]{0:T(128)}, u32[]{:S(2)}) copy-start(f32[20]{0:T(128)} %copy-done.11) | copy-start | bytes 244
  86.8 9.5 %copy-start.13 = (f32[20]{0:T(128)S(1)}, f32[20]{0:T(128)}, u32[]{:S(2)}) copy-start(f32[20]{0:T(128)} %slice_reduce_fusion.1) | copy-start | bytes 244
  86.8 9.5 %copy-start.15 = (f32[20]{0:T(128)S(1)}, f32[20]{0:T(128)}, u32[]{:S(2)}) copy-start(f32[20]{0:T(128)} %copy-done.14) | copy-start | bytes 244
  86.8 9.5 %copy-start.16 = (pred[256]{0:T(512)(128)(4,1)S(1)}, pred[256]{0:T(512)(128)(4,1)}, u32[]{:S(2)}) copy-start(pred[256]{0:T(512)(128)(4,1)} %get-tuple-element.159) | copy-start | bytes 772
  86.8 9.5 %copy-start.18 = (pred[256]{0:T(512)(128)(4,1)S(1)}, pred[256]{0:T(512)(128)(4,1)}, u32[]{:S(2)}) copy-start(pred[256]{0:T(512)(128)(4,1)} %compare_bitcast_fusion) | copy-start | bytes 772
  96.5 5.2 %copy-start.17 = (f32[20]{0:T(128)S(1)}, f32[20]{0:T(128)}, u32[]{:S(2)}) copy-start(f32[20]{0:T(128)} %get-tuple-element.148) | copy-start | bytes 244
  96.5 5.2 %copy-start.19 = (f32[20]{0:T(128)S(1)}, f32[20]{0:T(128)}, u32[]{:S(2)}) copy-start(f32[20]{0:T(128)} %get-tuple-element.156) | copy-start | bytes 244
  96.5 5.2 %copy-start = (f32[256,20,64]{0,2,1:T(8,128)S(1)}, f32[256,20,64]{0,2,1:T(8,128)}, u32[]{:S(2)}) copy-start(f32[256,20,64]{0,2,1:T(8,128)} %fusion.21) | copy-start | bytes 3932164
  96.5 5.2 %copy-start.4 = (bf16[256,128]{1,0:T(8,128)(2,1)S(1)}, bf16[256,128]{1,0:T(8,128)(2,1)}, u32[]{:S(2)}) copy-start(bf16[256,128]{1,0:T(8,128)(2,1)} %param.13) | copy-start | bytes 196612
Sparse Core Ops, SparseCore 0:
  101.8 30.7 all-reduce.2
where the time goes:
time: 142 us; the launch traced here: 141 us
  blocking collectives  45.5 us (32%)
  matrix products  24 us (17%)
  local copies, waits for them, and re-layouts  16.6 us (12%)
  between operations  15.8 us (11%)
  waiting for transfers between devices  14.6 us (10%)
  other arithmetic  12.4 us (9%)
  starting transfers between devices  11.9 us (8%)
    unnamed x1, blocking collectives  26.1 us
    psum x1, blocking collectives, body(): grad_rate = -lax.psum(rate_total, 'seq')  19.4 us
    psum x1, waiting for transfers between devices, body(): grad_input_map = lax.psum(grad_b_list[0], 'head')  9.15 us
    all_to_all x1, starting transfers between devices, body(): lax.all_to_all(sliced, 'seq', split_axis=1, concat_axis=1, tiled=True)  7.31 us
    mul x8, local copies, waits for them, and re-layouts, backward_step(): return (grad_piece + gain_piece[:, None] * running, running)  5.48 us
    all_to_all x1, waiting for transfers between devices, body(): lax.all_to_all(jnp.transpose(exclusive, (1, 0, 2)), 'seq', split_axis=1,...  5.48 us
    dot_general x1, matrix products, prepare(): jnp.einsum('shp,uhp->hsu', x_block, grad_block, preferred_element_type=jn...  5.34 us
    unnamed x51, local copies, waits for them, and re-layouts  5.26 us
  transfers between devices with their start and end apart: 3, of which 2 were waited for; matrix products, arithmetic and copies ran while one was open for 15% of the time, Pallas kernels for 0%

commit v1 on v0

--- a/solution.py
+++ b/solution.py
@@ -2,6 +2,7 @@
 import jax.numpy as jnp
 from jax import lax
 from jax.sharding import PartitionSpec as P
+from jax.lax import axis_size, ppermute
 
 highest = lax.Precision.HIGHEST
 
@@ -139,7 +140,15 @@
         rate_total = rate_part
         carried = prepared[1] + prepared[0][:, None, None] * carried
     grad_inputs = grad_x_list[0]
-    grad_input_map = lax.psum(grad_b_list[0], "head")
+    my_data = grad_b_list[0]
+    dev_count = axis_size("head")
+    grad_input_map, res = (my_data, 0)
+    while 1 << res < dev_count:
+        p_next = ppermute(
+            grad_input_map, "head", tuple(((q, q ^ 1 << res) for q in range(dev_count)))
+        )
+        grad_input_map = grad_input_map + p_next
+        res = res + 1
     grad_rate = -lax.psum(rate_total, "seq")
     return (grad_inputs, grad_input_map, grad_rate)
 

time: 142 us -> 122 us (0.86)
  between operations: 15.8 us -> 2.36 us
  waiting for transfers between devices: 14.6 us -> 5.97 us
  other arithmetic: 12.4 us -> 15.2 us
  starting transfers between devices: 11.9 us -> 13.5 us
    psum x1 -> x0, waiting for transfers between devices: 9.15 us -> none  [body(): grad_input_map = lax.psum(grad_b_list[0], 'head')]
    ppermute x0 -> x2, starting transfers between devices: none -> 1.63 us  [body(): ppermute(grad_input_map, 'head', tuple(((q, q ^ 1 << res) for q in range(...]
    unnamed x51 -> x52, local copies, waits for them, and re-layouts: 5.26 us -> 4.96 us
  transfers between devices with their start and end apart: 3 -> 4, of which waited for: 2 -> 2; matrix products, arithmetic and copies ran while one was open for 15% -> 20% of each run, Pallas kernels for 0% -> 0%
where the time goes in v1:
time: 122 us; the launch traced here: 121 us
  blocking collectives  44.3 us (36%)
  matrix products  23.3 us (19%)
  local copies, waits for them, and re-layouts  16.2 us (13%)
  other arithmetic  15.2 us (12%)
  starting transfers between devices  13.5 us (11%)
  waiting for transfers between devices  5.97 us (5%)
  between operations  2.36 us (2%)
    unnamed x1, blocking collectives  24.9 us
    psum x1, blocking collectives, body(): grad_rate = -lax.psum(rate_total, 'seq')  19.4 us
    all_to_all x1, starting transfers between devices, body(): lax.all_to_all(sliced, 'seq', split_axis=1, concat_axis=1, tiled=True)  7.31 us
    dot_general x1, matrix products, prepare(): jnp.einsum('shp,uhp->hsu', x_block, grad_block, preferred_element_type=jn...  6.19 us
    mul x8, local copies, waits for them, and re-layouts, backward_step(): return (grad_piece + gain_piece[:, None] * running, running)  5.48 us
    dynamic_update_slice x8, other arithmetic, body(): lax.scan(backward_step, jnp.zeros_like(received[:, 0]), (jnp.transpose(re...  5.13 us
    unnamed x52, local copies, waits for them, and re-layouts  4.96 us
    all_to_all x1, waiting for transfers between devices, body(): lax.all_to_all(jnp.transpose(exclusive, (1, 0, 2)), 'seq', split_axis=1,...  4.66 us
  transfers between devices with their start and end apart: 4, of which 2 were waited for; matrix products, arithmetic and copies ran while one was open for 20% of the time, Pallas kernels for 0%

profile of v1, /device:TPU:0, one launch (start us, length us, event | category | flops | bytes accessed | tf_op | source)
XLA Modules:
  0.0 121.0 jit_solution(13743856752084405102)
XLA Ops:
  1.4 0.7 neg.7
  2.1 0.8 reshape.290
  4.4 0.8 select_reduce_fusion
  5.2 0.9 copy.37
  6.1 1.4 %copy.36 = bf16[256,1280]{0,1:T(8,128)(2,1)S(1)} copy(bf16[256,1280]{1,0:T(8,128)(2,1)} %param.15) | data formatting | bytes 1310720 | tf_op args[5]
  7.5 1.7 %fusion.31 = f32[20,64,128]{2,1,0:T(8,128)S(1)} fusion(bf16[256,20,64]{0,2,1:T(8,128)(2,1)S(1)} %bitcast.80, f32[256,128]{0,1:T(8,128)S(1)} %copy.37, f32[20,256]{1,0:T(8,128)S(1)} %get-tuple-element.152, f32[20]{0:T(128)S(1)} %broadcast_multiply_fusion.1), kind=kOutput, calls=%fused_computation.38 | convolution fusion | flops 504135680 | bytes 1462352 | tf_op jit(solution)/shard_map/hun,uhp->hpn/dot_general | solution.py:35
  9.4 1.3 %copy.39 = f32[20,8,1024]{2,0,1:T(8,128)} copy(f32[20,8,1024]{2,1,0:T(8,128)S(1)} %reshape.293) | data formatting | bytes 1310720 | tf_op jit(solution)/shard_map/reshape | solution.py:116
  10.6 7.3 %all-to-all-start = ((f32[20,8,1024]{2,0,1:T(8,128)}), f32[20,8,1024]{2,0,1:T(8,128)S(1)}, u32[]{:S(2)}, u32[]{:S(2)}) async-start(f32[20,8,1024]{2,0,1:T(8,128)} %copy.39), calls=%async_computation | async-start | bytes 1572864 | tf_op jit(solution)/shard_map/all_to_all | solution.py:117
  17.9 1.3 %dynamic-slice = u32[1]{0:T(128)} dynamic-slice(u32[32]{0:T(128)} %constant.57, u32[]{:T(128)S(6)} %add.66), dynamic_slice_sizes={1} | dynamic-slice | bytes 12
  19.9 0.9 dynamic-update-slice
  20.7 24.9 %all-reduce = f32[160]{0:T(256)S(1)} all-reduce(f32[160]{0:T(256)S(1)} %dynamic-update-slice), channel_id=2, replica_groups=mesh['seq'=8,'head'=4] {'seq'}, use_global_device_ids=true, to_apply=%add | all-reduce | flops 160 | bytes 1280
  45.6 0.7 reshape.297
  46.3 1.5 %convert_element_type.21 = f32[256,128]{1,0:T(8,128)} convert(bf16[256,128]{1,0:T(8,128)(2,1)} %param.13) | non-fusion elementwise | flops 32768 | bytes 196608 | tf_op jit(solution)/shard_map/convert_element_type | solution.py:59
  48.7 0.7 slice_reduce_fusion.1
  49.4 1.4 %fusion.37 = pred[256,256]{1,0:T(8,128)(4,1)} fusion(pred[256]{0:T(512)(128)(4,1)} %copy-done.13), kind=kLoop, calls=%fused_computation.42 | loop fusion | flops 196608 | bytes 65792 | tf_op jit(solution)/shard_map/and | solution.py:17
  50.8 1.8 %fusion.43 = f32[256,256]{1,0:T(8,128)} fusion(bf16[256,128]{1,0:T(8,128)(2,1)} %param.13, bf16[256,128]{1,0:T(8,128)(2,1)} %param.14), kind=kOutput, calls=%fused_computation.64 | convolution fusion | flops 16777216 | bytes 393216 | tf_op jit(solution)/shard_map/dot_general | solution.py:20
  52.6 1.0 broadcast_in_dim.97
  53.6 11.4 %while.17 = (s32[]{:T(128)}, f32[20,1024]{1,0:T(8,128)S(1)}, f32[8,20,1024]{2,1,0:T(8,128)}, f32[8,20,1024]{2,1,0:T(8,128)S(1)}, f32[8,20]{1,0:T(8,128)}, /*index=5*/s32[]{:T(128)}, s32[]{:T(128)}, s32[]{:T(128)}) while((s32[]{:T(128)}, f32[20,1024]{1,0:T(8,128)S(1)}, f32[8,20,1024]{2,1,0:T(8,128)}, f32[8,20,1024]{2,1,0:T(8,128)S(1)}, ...), condition=%wide.region_3.4_spmd.clone, body=%wide.region_2.3_spmd.clone.sunk | while | flops 81924 | bytes 426352 | solution.py:119
  53.6 0.7 fusion.55
  54.3 0.6 bitcast_dynamic-update-slice_fusion.2
  55.0 0.7 fusion.55
  55.7 0.6 bitcast_dynamic-update-slice_fusion.2
  56.4 0.7 fusion.55
  57.9 0.7 fusion.55
  58.5 0.6 bitcast_dynamic-update-slice_fusion.2
  59.3 0.7 fusion.55
  60.0 0.6 bitcast_dynamic-update-slice_fusion.2
  60.7 0.7 fusion.55
  61.4 0.6 bitcast_dynamic-update-slice_fusion.2
  62.1 0.7 fusion.55
  62.8 0.6 bitcast_dynamic-update-slice_fusion.2
  63.6 0.7 fusion.55
  64.3 0.6 bitcast_dynamic-update-slice_fusion.2
  65.0 4.5 %all-to-all-start.1 = ((f32[20,8,1024]{2,0,1:T(8,128)}), f32[20,8,1024]{2,0,1:T(8,128)S(1)}, u32[]{:S(2)}, u32[]{:S(2)}) async-start(f32[20,8,1024]{2,0,1:T(8,128)} %bitcast.8), calls=%async_computation.1 | async-start | bytes 1572864 | tf_op jit(solution)/shard_map/all_to_all | solution.py:125
  69.5 2.8 %multiply_reduce_fusion.1 = f32[20,256]{1,0:T(8,128)} fusion(bf16[256,20,64]{0,2,1:T(8,128)(2,1)S(1)} %bitcast.81, f32[256,128]{0,1:T(8,128)} %copy-done.10, f32[1,20,64,128]{3,2,1,0:T(8,128)S(1)} %copy-done.2), kind=kOutput, calls=%fused_computation.17 | convolution fusion | flops 504622080 | bytes 1462272 | tf_op jit(solution)/shard_map/uhp,hpn->hun/dot_general | solution.py:36
  72.4 3.7 %fusion.21 = f32[256,20,64]{0,2,1:T(8,128)} fusion(bf16[256,20,64]{0,2,1:T(8,128)(2,1)S(1)} %bitcast.82, f32[256,256]{1,0:T(8,128)} %fusion.43, f32[20,256]{1,0:T(8,128)S(1)} %get-tuple-element.153, pred[256,256]{1,0:T(8,128)(4,1)} %fusion.37), kind=kOutput, calls=%fused_computation.29 | convolution fusion | flops 174325760 | bytes 2314240 | tf_op jit(solution)/shard_map/hsu,uhp->shp/dot_general | solution.py:25
  76.1 6.2 %multiply_reduce_fusion = (f32[20]{0:T(128)}, f32[20,256,256]{2,1,0:T(8,128)}) fusion(f32[20,256]{1,0:T(8,128)S(1)} %bitcast.87, f32[20,256]{1,0:T(8,128)S(1)} %copy-done.8, f32[256,256]{1,0:T(8,128)S(1)} %copy-done.7, f32[20,256]{1,0:T(8,128)} %copy-done.12, pred[256,256]{1,0:T(8,128)(4,1)S(1)} %copy-done.11, bf16[256,20,64]{0,2,1:T(8,128)(2,1)S(1)} %bitcast.76, ...), kind=kOutput, calls=%fused_computation.4 | convolution fusion | flops 179568624 | bytes 6942800 | tf_op jit(solution)/shard_map/shp,uhp->hsu/dot_general | solution.py:21
  82.3 4.7 %all-to-all-done.1 = f32[20,8,1024]{2,0,1:T(8,128)S(1)} async-done(((f32[20,8,1024]{2,0,1:T(8,128)}), f32[20,8,1024]{2,0,1:T(8,128)S(1)}, u32[]{:S(2)}, u32[]{:S(2)}) %all-to-all-start.1) | async-done | bytes 655392 | tf_op jit(solution)/shard_map/all_to_all | solution.py:125
  87.0 1.1 multiply_reduce_fusion.2
  88.2 1.9 %fusion.9 = (f32[20,256]{1,0:T(8,128)S(1)}, f32[20,128,256]{1,2,0:T(8,128)S(1)}) fusion(f32[256,128]{1,0:T(8,128)S(1)} %copy-done.4, f32[20,64,128]{2,1,0:T(8,128)S(1)} %reshape.294, bf16[256,20,64]{0,2,1:T(8,128)(2,1)S(1)} %bitcast.77), kind=kOutput, calls=%fused_computation.16 | convolution fusion | flops 504622080 | bytes 4083712 | tf_op jit(solution)/shard_map/shp,hpn->hsn/dot_general | solution.py:62
  90.1 1.0 multiply_reduce_fusion.4
  91.1 4.5 %fusion.8 = f32[256,128]{1,0:T(8,128)S(1)} fusion(f32[20,128,256]{1,2,0:T(8,128)S(1)} %get-tuple-element.155, f32[20,256]{1,0:T(8,128)S(1)} %get-tuple-element.150, f32[20,256]{1,0:T(8,128)} %param.11, f32[20,256,256]{2,1,0:T(8,128)} %get-tuple-element.157, f32[20,256]{1,0:T(8,128)} %copy-done.12, pred[256,256]{1,0:T(8,128)(4,1)} %fusion.37, ...), kind=kOutput, calls=%fused_computation.15 | convolution fusion | flops 344686592 | bytes 8187904 | tf_op jit(solution)/shard_map/hsu,un->hsn/dot_general | solution.py:26
  95.7 1.3 %collective-permute-done = f32[256,128]{1,0:T(8,128)S(1)} collective-permute-done((f32[256,128]{1,0:T(8,128)S(1)}, f32[256,128]{1,0:T(8,128)S(1)}, u32[]{:S(2)}, u32[]{:S(2)}) %collective-permute-start) | collective-permute-done | bytes 131104 | tf_op jit(solution)/shard_map/ppermute | solution.py:147
  97.1 1.6 %collective-permute-start.1 = (f32[256,128]{1,0:T(8,128)S(1)}, f32[256,128]{1,0:T(8,128)S(1)}, u32[]{:S(2)}, u32[]{:S(2)}) collective-permute-start(f32[256,128]{1,0:T(8,128)S(1)} %add.61), channel_id=1, source_target_pairs={{0,2},{1,3},{2,0},{3,1},{4,6},{5,7},{6,4},{7,5},{8,10},{9,11},{10,... | collective-permute-start | bytes 393224 | tf_op jit(solution)/shard_map/ppermute | solution.py:147
  98.6 0.7 fusion.25
  99.3 19.4 %psum.7 = f32[20]{0:T(128)S(1)} all-reduce(f32[20]{0:T(128)S(1)} %multiply_add_fusion), channel_id=1, replica_groups=mesh['seq'=8,'head'=4] {'seq'}, use_global_device_ids=true, to_apply=%region_11.12 | all-reduce | flops 20 | bytes 160 | tf_op jit(solution)/shard_map/psum | solution.py:152
  118.7 1.1 copy.44
  120.3 0.7 add.62
  (78 shorter events, 4.6 us)
Async XLA Ops:
  0.6 47.2 %copy-start.1 = (bf16[256,1280]{1,0:T(8,128)(2,1)S(1)}, bf16[256,1280]{1,0:T(8,128)(2,1)}, u32[]{:S(2)}) copy-start(bf16[256,1280]{1,0:T(8,128)(2,1)} %param.10) | copy-start | bytes 1966084
  0.6 47.4 %copy-start.2 = (f32[1,20,64,128]{3,2,1,0:T(8,128)S(1)}, f32[1,20,64,128]{3,2,1,0:T(8,128)}, u32[]{:S(2)}) copy-start(f32[1,20,64,128]{3,2,1,0:T(8,128)} %param.16) | copy-start | bytes 1966084
  2.1 2.3 %copy-start.17 = (f32[20]{0:T(128)}, f32[20]{0:T(128)S(1)}, u32[]{:S(2)}) copy-start(f32[20]{0:T(128)S(1)} %neg.7) | copy-start | bytes 244
  3.8 44.9 %copy-start.5 = (f32[3,8,2,128]{3,1,2,0:T(8,128)}, f32[3,8,2,128]{3,1,2,0:T(8,128)S(1)}, u32[]{:S(2)}) copy-start(f32[3,8,2,128]{3,1,2,0:T(8,128)S(1)} %copy.47) | copy-start | bytes 73732
  4.3 3.2 %copy-start.13 = (pred[256]{0:T(512)(128)(4,1)}, pred[256]{0:T(512)(128)(4,1)S(1)}, u32[]{:S(2)}) copy-start(pred[256]{0:T(512)(128)(4,1)S(1)} %get-tuple-element.158) | copy-start | bytes 772
  4.4 68.0 %copy-start.12 = (f32[20,256]{1,0:T(8,128)}, f32[20,256]{1,0:T(8,128)S(1)}, u32[]{:S(2)}) copy-start(f32[20,256]{1,0:T(8,128)S(1)} %get-tuple-element.153) | copy-start | bytes 61444
  5.1 2.4 %copy-start.14 = (f32[20]{0:T(128)}, f32[20]{0:T(128)S(1)}, u32[]{:S(2)}) copy-start(f32[20]{0:T(128)S(1)} %get-tuple-element.137) | copy-start | bytes 244
  6.1 4.5 %copy-start.10 = (f32[256,128]{0,1:T(8,128)}, f32[256,128]{0,1:T(8,128)S(1)}, u32[]{:S(2)}) copy-start(f32[256,128]{0,1:T(8,128)S(1)} %copy.37) | copy-start | bytes 393220
  10.6 42.0 %all-to-all-start = ((f32[20,8,1024]{2,0,1:T(8,128)}), f32[20,8,1024]{2,0,1:T(8,128)S(1)}, u32[]{:S(2)}, u32[]{:S(2)}) async-start(f32[20,8,1024]{2,0,1:T(8,128)} %copy.39), calls=%async_computation | async-start | bytes 1572864 | tf_op jit(solution)/shard_map/all_to_all | solution.py:117
  65.0 22.0 %all-to-all-start.1 = ((f32[20,8,1024]{2,0,1:T(8,128)}), f32[20,8,1024]{2,0,1:T(8,128)S(1)}, u32[]{:S(2)}, u32[]{:S(2)}) async-start(f32[20,8,1024]{2,0,1:T(8,128)} %bitcast.8), calls=%async_computation.1 | async-start | bytes 1572864 | tf_op jit(solution)/shard_map/all_to_all | solution.py:125
  72.3 3.7 %copy-start.6 = (f32[3,8,2,128]{3,1,2,0:T(8,128)S(1)}, f32[3,8,2,128]{3,1,2,0:T(8,128)}, u32[]{:S(2)}) copy-start(f32[3,8,2,128]{3,1,2,0:T(8,128)} %copy-done.5) | copy-start | bytes 73732
  72.3 3.7 %copy-start.7 = (f32[256,256]{1,0:T(8,128)S(1)}, f32[256,256]{1,0:T(8,128)}, u32[]{:S(2)}) copy-start(f32[256,256]{1,0:T(8,128)} %fusion.43) | copy-start | bytes 786436
  72.4 3.7 %copy-start.8 = (f32[20,256]{1,0:T(8,128)S(1)}, f32[20,256]{1,0:T(8,128)}, u32[]{:S(2)}) copy-start(f32[20,256]{1,0:T(8,128)} %param.11) | copy-start | bytes 61444
  72.4 3.7 %copy-start.11 = (pred[256,256]{1,0:T(8,128)(4,1)S(1)}, pred[256,256]{1,0:T(8,128)(4,1)}, u32[]{:S(2)}) copy-start(pred[256,256]{1,0:T(8,128)(4,1)} %fusion.37) | copy-start | bytes 196612
  76.1 12.0 %copy-start.4 = (f32[256,128]{1,0:T(8,128)S(1)}, f32[256,128]{1,0:T(8,128)}, u32[]{:S(2)}) copy-start(f32[256,128]{1,0:T(8,128)} %convert_element_type.21) | copy-start | bytes 393220
  82.3 7.7 %copy-start.15 = (f32[20]{0:T(128)S(1)}, f32[20]{0:T(128)}, u32[]{:S(2)}) copy-start(f32[20]{0:T(128)} %copy-done.14) | copy-start | bytes 244
  82.3 7.7 %copy-start.16 = (f32[20]{0:T(128)S(1)}, f32[20]{0:T(128)}, u32[]{:S(2)}) copy-start(f32[20]{0:T(128)} %slice_reduce_fusion.1) | copy-start | bytes 244
  82.3 7.7 %copy-start.18 = (f32[20]{0:T(128)S(1)}, f32[20]{0:T(128)}, u32[]{:S(2)}) copy-start(f32[20]{0:T(128)} %copy-done.17) | copy-start | bytes 244
  82.3 7.8 %copy-start.19 = (pred[256]{0:T(512)(128)(4,1)S(1)}, pred[256]{0:T(512)(128)(4,1)}, u32[]{:S(2)}) copy-start(pred[256]{0:T(512)(128)(4,1)} %get-tuple-element.159) | copy-start | bytes 772
  91.1 4.6 %copy-start.20 = (f32[20]{0:T(128)S(1)}, f32[20]{0:T(128)}, u32[]{:S(2)}) copy-start(f32[20]{0:T(128)} %get-tuple-element.148) | copy-start | bytes 244
  91.1 4.6 %copy-start.21 = (f32[20]{0:T(128)S(1)}, f32[20]{0:T(128)}, u32[]{:S(2)}) copy-start(f32[20]{0:T(128)} %get-tuple-element.156) | copy-start | bytes 244
  91.1 7.5 %copy-start = (f32[256,20,64]{0,2,1:T(8,128)S(1)}, f32[256,20,64]{0,2,1:T(8,128)}, u32[]{:S(2)}) copy-start(f32[256,20,64]{0,2,1:T(8,128)} %fusion.21) | copy-start | bytes 3932164
  91.1 7.5 %copy-start.3 = (bf16[256,128]{1,0:T(8,128)(2,1)S(1)}, bf16[256,128]{1,0:T(8,128)(2,1)}, u32[]{:S(2)}) copy-start(bf16[256,128]{1,0:T(8,128)(2,1)} %param.13) | copy-start | bytes 196612
  91.1 7.5 %copy-start.9 = (f32[20,256]{1,0:T(8,128)S(1)}, f32[20,256]{1,0:T(8,128)}, u32[]{:S(2)}) copy-start(f32[20,256]{1,0:T(8,128)} %param.11) | copy-start | bytes 61444
  95.6 1.4 %collective-permute-start = (f32[256,128]{1,0:T(8,128)S(1)}, f32[256,128]{1,0:T(8,128)S(1)}, u32[]{:S(2)}, u32[]{:S(2)}) collective-permute-start(f32[256,128]{1,0:T(8,128)S(1)} %fusion.8), channel_id=1, source_target_pairs={{0,1},{1,0},{2,3},{3,2},{4,5},{5,4},{6,7},{7,6},{8,9},{9,8},{10,11... | collective-permute-start | bytes 393224 | tf_op jit(solution)/shard_map/ppermute | solution.py:147
  97.1 23.3 %collective-permute-start.1 = (f32[256,128]{1,0:T(8,128)S(1)}, f32[256,128]{1,0:T(8,128)S(1)}, u32[]{:S(2)}, u32[]{:S(2)}) collective-permute-start(f32[256,128]{1,0:T(8,128)S(1)} %add.61), channel_id=1, source_target_pairs={{0,2},{1,3},{2,0},{3,1},{4,6},{5,7},{6,4},{7,5},{8,10},{9,11},{10,... | collective-permute-start | bytes 393224 | tf_op jit(solution)/shard_map/ppermute | solution.py:147
